TPU v7x, 32 devices: a whole 2x2x4 slice. The times are simulated.
32 devices in a mesh: seq: 16 (over z, y, core), batch: 2 (over x).
Axes of the slice: x: 2, y: 2, z: 4, core: 2. Of those that a mesh axis runs over, the one named last changes fastest.
Arguments:
- hidden_in: bfloat16 [2, 4096, 2304], P('batch', 'seq'), may hold values from -6 to 6
- segment_ids: int32 [2, 4096], P('batch', 'seq'), may hold values from 0 to 15, never falling along the last dimension, each value on 1 to 512 neighbouring positions
- pre_gain: float32 [2304], replicated, may hold values from 0.25 to 1.75
- w_qkv: bfloat16 [2304, 2048], P('seq'), may hold values from -0.27083333 to 0.27083333
- w_out: bfloat16 [1024, 2304], P('seq'), may hold values from -0.1875 to 0.1875
- post_gain: float32 [2304], replicated, may hold values from 0.25 to 1.75
Outputs:
- layer_out: bfloat16 [2, 4096, 2304], P('batch', 'seq')
Inputs may be any that keep to these rules, and one draw needn't show every extreme that they name: `segment_ids`: along each sequence the numbers never fall; a document is 1 to 512 positions long, and each sequence has one of exactly 512.
All inputs are finite; a program needn't handle non-finite values.
Results may differ from a plain program's by a relative error of at most 0.012.
The roundings to bfloat16 on the way count: a program that leaves them out, or rounds other values in their place, can miss the bound.
Values may be sent and summed in bfloat16 or wider, within the bound.
A program may use at most 128 MiB of HBM per device.

v0:
```python
import functools
import math

import jax
import jax.numpy as jnp
from jax import lax
from jax.experimental import pallas as pl
from jax.experimental.pallas import tpu as pltpu
from jax.sharding import PartitionSpec as P

Q_HEADS = 4
KV_HEADS = 2
HEAD = 256
WINDOW = 4096
DOCS = 16


EPS = 1e-06
CAP = 50.0


def from_behind(block, axis, distance):
    devices = range(lax.axis_size(axis))
    route = [(i - distance, i) for i in devices if i - distance in devices]
    return lax.ppermute(block, axis, route)


def rms_scale(values, gain):
    return values * lax.rsqrt(jnp.mean(values * values, axis=-1, keepdims=True) + EPS) * gain


def rotary(values, positions, leading):
    head_size = values.shape[-1]
    half_dim = head_size // 2
    inverse = 1.0 / 10000.0 ** (jnp.arange(half_dim, dtype=jnp.float32) * 2.0 / head_size)
    angles = positions.astype(jnp.float32)[:, None] * inverse[None, :]
    shape = (
        (1,) * leading + (positions.shape[0],) + (1,) * (values.ndim - 2 - leading) + (half_dim,)
    )
    cosine = jnp.cos(angles).reshape(shape)
    sine = jnp.sin(angles).reshape(shape)
    first_half = values[..., :half_dim]
    second_half = values[..., half_dim:]
    return jnp.concatenate(
        [first_half * cosine - second_half * sine, second_half * cosine + first_half * sine],
        axis=-1,
    )


def plain_layer(hidden_in, segment_ids, pre_gain, w_qkv, w_out, post_gain):
    tok_rows = hidden_in.shape[1]
    seq_count = lax.axis_size("seq")
    seq_index = lax.axis_index("seq")
    groups = Q_HEADS // KV_HEADS
    doc_most = min(WINDOW, seq_count * tok_rows // 8)
    hops = min(-(-(doc_most - 1) // tok_rows), seq_count - 1)
    positions = seq_index * tok_rows + jnp.arange(tok_rows, dtype=jnp.int32)
    own_ids = segment_ids[0]
    id_blocks = [from_behind(own_ids, "seq", d) for d in range(hops, 0, -1)] + [own_ids]
    widened = hidden_in[0].astype(jnp.float32)
    normed = rms_scale(widened, pre_gain).astype(jnp.bfloat16)
    projected = jnp.dot(
        normed,
        lax.all_gather(w_qkv, "seq", axis=0, tiled=True),
        preferred_element_type=jnp.float32,
    )
    queries = rotary(
        projected[:, : Q_HEADS * HEAD].reshape(tok_rows, KV_HEADS, groups, HEAD), positions, 0
    ).astype(jnp.bfloat16)
    key_rows = rotary(
        projected[:, Q_HEADS * HEAD : (Q_HEADS + KV_HEADS) * HEAD].reshape(
            tok_rows, KV_HEADS, HEAD
        ),
        positions,
        0,
    ).astype(jnp.bfloat16)
    value_rows = projected[:, (Q_HEADS + KV_HEADS) * HEAD :].astype(jnp.bfloat16)
    both = jnp.concatenate([key_rows.reshape(tok_rows, KV_HEADS * HEAD), value_rows], axis=1)
    blocks = [from_behind(both, "seq", d) for d in range(hops, 0, -1)] + [both]
    kv = jnp.concatenate(blocks, axis=0).reshape(-1, 2, KV_HEADS, HEAD)
    ids = jnp.concatenate(id_blocks, axis=0)
    key_pos = (seq_index - hops) * tok_rows + jnp.arange((hops + 1) * tok_rows, dtype=jnp.int32)
    allowed = (
        (key_pos[None, :] >= 0)
        & (key_pos[None, :] <= positions[:, None])
        & (positions[:, None] - key_pos[None, :] < WINDOW)
        & (ids[None, :] == own_ids[:, None])
    )
    scores = jnp.einsum(
        "qhgd,khd->hgqk", queries, kv[:, 0], preferred_element_type=jnp.float32
    ) * (1.0 / math.sqrt(HEAD))
    capped = CAP * jnp.tanh(scores / CAP)
    weights = jnp.where(allowed[None, None], jnp.exp(capped), 0.0)
    totals = jnp.sum(weights, axis=-1)
    mixed = jnp.einsum(
        "hgqk,khd->hgqd", weights.astype(jnp.bfloat16), kv[:, 1], preferred_element_type=jnp.float32
    )
    attended = (mixed / totals[..., None]).astype(jnp.bfloat16)
    attended = attended.transpose(2, 0, 1, 3).reshape(tok_rows, Q_HEADS * HEAD)
    branch = jnp.dot(
        attended,
        lax.all_gather(w_out, "seq", axis=0, tiled=True),
        preferred_element_type=jnp.float32,
    )
    return (widened + rms_scale(branch, post_gain)).astype(jnp.bfloat16)[None]


class Gather:
    def __init__(self, place, own_ref, full_ref, piece, send_sems, recv_sems):
        self.place, self.own_ref, self.full_ref = place, own_ref, full_ref
        self.piece, self.send_sems, self.recv_sems = piece, send_sems, recv_sems
        self.steps = place["chips"] - 1
        self.started = []

    def slot(self, kind, hop, unit):
        return (kind * self.steps + hop - 1) * 2 + unit

    def spot(self, kind, hop, core, unit):
        place = self.place
        shift = -hop if kind == 0 else hop
        third = (1, 2 * place["x"], 2 - 2 * place["x"])[kind]
        device = place["chip_at"](place["ring"] + shift) * 2 + core
        return self.piece(self.full_ref, device, third, unit)

    def copy(self, source, target, slot, device):
        return pltpu.make_async_remote_copy(
            src_ref=source,
            dst_ref=target,
            send_sem=self.send_sems.at[slot],
            recv_sem=self.recv_sems.at[slot],
            device_id=device,
            device_id_type=pl.DeviceIdType.MESH,
        )

    def send(self, source, target, slot, device):
        moving = self.copy(source, target, slot, device)
        moving.start()
        self.started.append(moving)

    def arrived(self, spot, slot):
        self.copy(spot, spot, slot, self.place["sibling"]).wait_recv()

    def first_hop(self):
        place = self.place
        for unit in (1, 0):
            if unit == 0:
                for moving in self.started[-2:]:
                    moving.wait_send()
                del self.started[-2:]
            for kind, target in ((0, place["up"]), (1, place["down"])):
                third = (1, 2 * place["x"])[kind]
                self.send(
                    self.piece(self.own_ref, 0, third, unit),
                    self.piece(self.full_ref, place["seq"], third, unit),
                    self.slot(kind, 1, unit),
                    target,
                )

    def share_own(self):
        rows = self.own_ref.shape[0]
        mine = self.full_ref.at[pl.ds(pl.multiple_of(self.place["seq"] * rows, 16), rows), :]
        self.send(self.own_ref, mine, 12 * self.steps, self.place["sibling"])

    def relay(self, kind, hop, unit):
        spot = self.spot(kind, hop, self.place["core"], unit)
        self.send(spot, spot, self.slot(kind + 3, hop, unit), self.place["sibling"])

    def take_x(self, hop, units=(1, 0)):
        for unit in units:
            self.arrived(self.spot(2, hop, self.place["core"], unit), self.slot(2, hop, unit))
            self.relay(2, hop, unit)

    def step(self, hop):
        place = self.place
        for unit in (1, 0):
            if hop > 1:
                self.take_x(hop - 1, (unit,))
            for kind, target in ((0, place["up"]), (1, place["down"])):
                spot = self.spot(kind, hop, place["core"], unit)
                self.arrived(spot, self.slot(kind, hop, unit))
                if hop < self.steps:
                    self.send(spot, spot, self.slot(kind, hop + 1, unit), target)
                if kind == 1:
                    self.send(spot, spot, self.slot(2, hop, unit), place["across"])
                self.relay(kind, hop, unit)

    def finish(self, units=(1, 0)):
        self.take_x(self.steps, units)
        other = 1 - self.place["core"]
        for unit in units:
            for hop in range(1, self.steps + 1):
                for kind in range(3):
                    self.arrived(self.spot(kind, hop, other, unit), self.slot(kind + 3, hop, unit))
        if 1 not in units:
            return
        rows = self.own_ref.shape[0]
        start = (self.place["seq"] + 1 - 2 * self.place["core"]) * rows
        theirs = self.full_ref.at[pl.ds(pl.multiple_of(start, 16), rows), :]
        self.arrived(theirs, 12 * self.steps)

    def drain(self):
        for moving in self.started:
            moving.wait_send()


def make_piece(rows, width, by_rows):
    def piece(ref, device, third, unit):
        if by_rows:
            part, columns = rows // 3, width // 2
            return ref.at[
                pl.ds(pl.multiple_of(device * rows + third * part, 16), part),
                pl.ds(unit * columns, columns),
            ]
        columns = width // 6
        return ref.at[
            pl.ds(pl.multiple_of(device * rows, 16), rows),
            pl.ds(pl.multiple_of(third * 2 * columns + unit * columns, 128), columns),
        ]

    return piece


def layer_kernel(
    chips, hid, ids_row, ids_col, cos, sin, pre, w_qkv, w_out, post, out,
    wq, wo, nrm, qry, kv, kv1, kv2, id1, id2, acc, tot, att, branch,
    q_send, q_recv, o_send, o_recv, s_send, s_recv, local_sem,
):
    seq, x = lax.axis_index("seq"), lax.axis_index("batch")
    chip, core = seq // 2, seq % 2
    half = chips // 2
    layer, side = chip // 2, chip % 2
    ring = (1 - side) * layer + side * (chips - 1 - layer)

    def chip_at(position):
        position = (position + chips) % chips
        far = position // half
        return (1 - far) * 2 * position + far * (2 * (chips - 1 - position) + 1)

    def at(device_chip, device_core, batch):
        return {"seq": device_chip * 2 + device_core, "batch": batch}

    place = dict(
        chips=chips, seq=seq, x=x, core=core, ring=ring, chip_at=chip_at,
        sibling=at(chip, 1 - core, x), across=at(chip, core, 1 - x),
        up=at(chip_at(ring + 1), core, x), down=at(chip_at(ring - 1), core, x),
    )
    after = at((chip + 1) % chips, core, x)
    before = at((chip + chips - 1) % chips, core, x)
    met = [place["sibling"], place["across"], place["up"], place["down"], after, before]
    barrier = pltpu.get_barrier_semaphore()
    for other in met:
        pl.semaphore_signal(barrier, 1, device_id=other, device_id_type=pl.DeviceIdType.MESH)
    pl.semaphore_wait(barrier, len(met))

    gather_q = Gather(place, w_qkv, wq, make_piece(*w_qkv.shape, True), q_send, q_recv)
    gather_o = Gather(place, w_out, wo, make_piece(*w_out.shape, False), o_send, o_recv)
    gather_q.share_own()
    gather_o.share_own()
    gather_q.first_hop()
    own_copies = []
    for index, (source, full) in enumerate(((w_qkv, wq), (w_out, wo))):
        rows = source.shape[0]
        mine = full.at[pl.ds(pl.multiple_of(seq * rows, 16), rows), :]
        own_copies.append(pltpu.make_async_copy(source, mine, local_sem.at[index]))
        own_copies[-1].start()

    def small(source, target, slot, device):
        return pltpu.make_async_remote_copy(
            src_ref=source, dst_ref=target, send_sem=s_send.at[slot], recv_sem=s_recv.at[slot],
            device_id=device, device_id_type=pl.DeviceIdType.MESH,
        )

    ids_on = small(ids_row, id2, 0, after)
    ids_on.start()

    tokens, width = hid.shape
    strip = 16

    @pl.loop(0, tokens // strip)
    def _(index):
        rows = pl.ds(pl.multiple_of(index * strip, strip), strip)
        nrm[rows, :] = rms_scale(hid[rows, :].astype(jnp.float32), pre[...]).astype(jnp.bfloat16)

    ids_on.wait()

    def pass_on(own, far, near, slot):
        @pl.when(core == 0)
        def _():
            small(own, near, slot, place["sibling"]).start()

        @pl.when(core == 1)
        def _():
            small(far, near, slot, place["sibling"]).start()

    pass_on(ids_row, id2, id1, 1)

    for hop in range(1, chips):
        gather_q.step(hop)
        if hop == 1:
            gather_o.first_hop()
        elif hop > 1:
            gather_o.step(hop - 1)
    gather_q.finish((1,))
    for moving in own_copies:
        moving.wait()

    def project(column):
        return jnp.dot(
            nrm[...], wq[:, column : column + HEAD], preferred_element_type=jnp.float32
        )

    def turned(values):
        a, b = values[:, : HEAD // 2], values[:, HEAD // 2 :]
        c, s = cos[...], sin[...]
        return jnp.concatenate([a * c - b * s, b * c + a * s], axis=1).astype(jnp.bfloat16)

    keys_at = Q_HEADS * HEAD
    for head in range(KV_HEADS):
        columns = slice(head * HEAD, (head + 1) * HEAD)
        kv[:, columns] = turned(project(keys_at + head * HEAD))
    for head in range(KV_HEADS, 2 * KV_HEADS):
        columns = slice(head * HEAD, (head + 1) * HEAD)
        kv[:, columns] = project(keys_at + head * HEAD).astype(jnp.bfloat16)
    kv_on = small(kv, kv2, 2, after)
    kv_on.start()
    for hop in range(chips - 1, chips):
        gather_o.step(hop)
    gather_q.finish((0,))
    for head in range(Q_HEADS):
        columns = slice(head * HEAD, (head + 1) * HEAD)
        qry[:, columns] = turned(project(head * HEAD))

    def block(head, source, allowed, first):
        group = head // (Q_HEADS // KV_HEADS)
        columns = slice(head * HEAD, (head + 1) * HEAD)
        keys = source[:, group * HEAD : (group + 1) * HEAD]
        values = source[:, (KV_HEADS + group) * HEAD : (KV_HEADS + group + 1) * HEAD]
        scores = lax.dot_general(
            qry[:, columns], keys, (((1,), (1,)), ((), ())), preferred_element_type=jnp.float32
        )
        capped = CAP * jnp.tanh(scores * (1.0 / (math.sqrt(HEAD) * CAP)))
        weights = jnp.where(allowed, jnp.exp(capped), 0.0)
        total = jnp.sum(weights, axis=1, keepdims=True)
        mixed = jnp.dot(weights.astype(jnp.bfloat16), values, preferred_element_type=jnp.float32)
        if first:
            acc[:, columns] = mixed
            tot[:, head * 128 : (head + 1) * 128] = jnp.broadcast_to(total, (tokens, 128))
        else:
            acc[:, columns] += mixed
            tot[:, head * 128 : (head + 1) * 128] += jnp.broadcast_to(total, (tokens, 128))

    query_ids = ids_col[:, :1]
    row = lax.broadcasted_iota(jnp.int32, (tokens, tokens), 0)
    column = lax.broadcasted_iota(jnp.int32, (tokens, tokens), 1)
    own_allowed = (column <= row) & (query_ids == ids_row[:1, :])
    for head in range(Q_HEADS):
        block(head, kv, own_allowed, True)
    small(ids_row, id1, 1, place["sibling"]).wait()
    kv_on.wait()
    pass_on(kv, kv2, kv1, 3)
    far_allowed = (query_ids == id2[:1, :]) & (row + seq >= row + 2)
    for head in range(Q_HEADS):
        block(head, kv2, far_allowed, False)
    small(kv, kv1, 3, place["sibling"]).wait()
    near_allowed = (query_ids == id1[:1, :]) & (row + seq >= row + 1)
    for head in range(Q_HEADS):
        block(head, kv1, near_allowed, False)
        columns = slice(head * HEAD, (head + 1) * HEAD)
        att[:, columns] = (acc[:, columns] / tot[:, head * 128 : head * 128 + 1]).astype(
            jnp.bfloat16
        )
    gather_o.finish()
    for start in range(0, width, 256):
        branch[:, start : start + 256] = jnp.dot(
            att[...], wo[:, start : start + 256], preferred_element_type=jnp.float32
        )

    @pl.loop(0, tokens // strip)
    def _(index):
        rows = pl.ds(pl.multiple_of(index * strip, strip), strip)
        scaled = rms_scale(branch[rows, :], post[...])
        out[rows, :] = (hid[rows, :].astype(jnp.float32) + scaled).astype(jnp.bfloat16)

    gather_q.drain()
    gather_o.drain()


def ring_layer(hidden_in, segment_ids, pre_gain, w_qkv, w_out, post_gain):
    tokens, width = hidden_in.shape[1:]
    seq_count = lax.axis_size("seq")
    chips = seq_count // 2
    positions = lax.axis_index("seq") * tokens + jnp.arange(tokens, dtype=jnp.int32)
    inverse = 1.0 / 10000.0 ** (jnp.arange(HEAD // 2, dtype=jnp.float32) * 2.0 / HEAD)
    angles = positions.astype(jnp.float32)[:, None] * inverse[None, :]
    ids = segment_ids[0]
    pieces = 12 * (chips - 1) + 1
    bf16, f32 = jnp.bfloat16, jnp.float32
    vmem, dma = pltpu.VMEM, pltpu.SemaphoreType.DMA
    heads = Q_HEADS * HEAD
    pairs = 2 * KV_HEADS * HEAD
    result = pl.pallas_call(
        functools.partial(layer_kernel, chips),
        out_shape=jax.ShapeDtypeStruct((tokens, width), bf16),
        in_specs=[pl.BlockSpec(memory_space=vmem)] * 9,
        out_specs=pl.BlockSpec(memory_space=vmem),
        scratch_shapes=[
            vmem((width, w_qkv.shape[1]), bf16),
            vmem((heads, width), bf16),
            vmem((tokens, width), bf16),
            vmem((tokens, heads), bf16),
            vmem((tokens, pairs), bf16),
            vmem((tokens, pairs), bf16),
            vmem((tokens, pairs), bf16),
            vmem((1, tokens), jnp.int32),
            vmem((1, tokens), jnp.int32),
            vmem((tokens, heads), f32),
            vmem((tokens, Q_HEADS * 128), f32),
            vmem((tokens, heads), bf16),
            vmem((tokens, width), f32),
            dma((pieces,)),
            dma((pieces,)),
            dma((pieces,)),
            dma((pieces,)),
            dma((4,)),
            dma((4,)),
            dma((2,)),
        ],
        compiler_params=pltpu.CompilerParams(
            collective_id=0, has_side_effects=True, vmem_limit_bytes=58 * 1024 * 1024
        ),
    )(
        hidden_in[0],
        segment_ids,
        jnp.broadcast_to(ids[:, None], (tokens, 128)),
        jnp.cos(angles),
        jnp.sin(angles),
        pre_gain,
        w_qkv,
        w_out,
        post_gain,
    )
    return result[None]


def per_device(hidden_in, segment_ids, pre_gain, w_qkv, w_out, post_gain):
    tokens = hidden_in.shape[1]
    seq_count = lax.axis_size("seq")
    doc_most = min(WINDOW, seq_count * tokens // 8)
    whole_tiles = w_qkv.shape[0] % 48 == 0 and w_out.shape[0] % 16 == 0
    two_hops = doc_most - 1 <= 2 * tokens and 3 * tokens <= WINDOW
    if whole_tiles and two_hops and seq_count % 4 == 0 and seq_count > 12 and lax.axis_size("batch") == 2:
        layer = ring_layer
    else:
        layer = plain_layer
    return layer(hidden_in, segment_ids, pre_gain, w_qkv, w_out, post_gain)


def solution(mesh):
    placed = (P("batch", "seq", None), P("batch", "seq"), P(), P("seq", None), P("seq", None), P())
    return jax.shard_map(
        per_device, mesh=mesh, in_specs=placed, out_specs=P("batch", "seq", None), check_vma=False
    )
```

profile of v0, /device:TPU:0, one launch (start us, length us, event | category | flops | bytes accessed | tf_op | source)
XLA Modules:
  0.0 88.3 jit_solution(9649584656294233656)
XLA Ops:
  0.0 1.4 %broadcast_in_dim.13.ids_col = s32[256,128]{1,0:T(8,128)} broadcast(s32[256]{0:T(256)} %bitcast.5), dimensions={0} | broadcast | bytes 132096 | tf_op jit(solution)/shard_map/broadcast_in_dim | solution.py:434
  1.5 1.2 %multiply_sine_fusion = (f32[256,128]{1,0:T(8,128)}, f32[256,128]{1,0:T(8,128)}) fusion(f32[128]{0:T(128)S(1)} %negate_power_fusion, f32[256]{0:T(256)S(1)} %add_convert_fusion), kind=kLoop, calls=%fused_computation | loop fusion | flops 32768 | bytes 263680 | tf_op jit(solution)/shard_map/sin | solution.py:436
  2.7 83.2 %shard_map.64 = bf16[256,2304]{1,0:T(8,128)(2,1)} custom-call(bf16[256,2304]{1,0:T(8,128)(2,1)} %bitcast.4, s32[1,256]{1,0:T(1,128)} %ids_row.1, s32[256,128]{1,0:T(8,128)} %broadcast_in_dim.13.ids_col, f32[256,128]{1,0:T(8,128)} %get-tuple-element.6.cos, f32[256,128]{1,0:T(8,128)} %get-tuple-element.5.sin, f32[2304]{0:T(1024)} %pre.1, ...), custom_call_target="tpu_custom_call" | custom-call | tf_op jit(solution)/shard_map/pallas_call | solution.py:401
  85.9 2.4 %copy.8 = bf16[1,256,2304]{2,1,0:T(8,128)(2,1)} copy(bf16[1,256,2304]{2,1,0:T(8,128)(2,1)} %bitcast.3) | data formatting | bytes 2359296
  (2 shorter events, 0.0 us)
where the time goes:
time: 88.5 us; the launch traced here: 88.3 us
  Pallas kernels  83.2 us (94%)
  local copies, waits for them, and re-layouts  3.8 us (4%)
  other arithmetic  1.26 us (1%)
    pallas_call x1, Pallas kernels, ring_layer(): pl.pallas_call(functools.partial(layer_kernel, chips), out_shape=jax.Shap...  83.2 us
    unnamed x1, local copies, waits for them, and re-layouts  2.36 us

commit v1 on v0

v1 whole, which is shorter than its diff:
```python
import functools
import math

import jax
import jax.numpy as jnp
import numpy as np
from jax import lax
from jax.experimental import pallas as pl
from jax.experimental.pallas import tpu as pltpu
from jax.sharding import PartitionSpec as P

Q_HEADS = 4
KV_HEADS = 2
HEAD = 256
WINDOW = 4096
DOCS = 16


EPS = 1e-06
CAP = 50.0


def from_behind(block, axis, distance):
    devices = range(lax.axis_size(axis))
    route = [(i - distance, i) for i in devices if i - distance in devices]
    return lax.ppermute(block, axis, route)


def rms_scale(values, gain):
    return values * lax.rsqrt(jnp.mean(values * values, axis=-1, keepdims=True) + EPS) * gain


def rotary(values, positions, leading):
    head_size = values.shape[-1]
    half_dim = head_size // 2
    inverse = 1.0 / 10000.0 ** (jnp.arange(half_dim, dtype=jnp.float32) * 2.0 / head_size)
    angles = positions.astype(jnp.float32)[:, None] * inverse[None, :]
    shape = (
        (1,) * leading + (positions.shape[0],) + (1,) * (values.ndim - 2 - leading) + (half_dim,)
    )
    cosine = jnp.cos(angles).reshape(shape)
    sine = jnp.sin(angles).reshape(shape)
    first_half = values[..., :half_dim]
    second_half = values[..., half_dim:]
    return jnp.concatenate(
        [first_half * cosine - second_half * sine, second_half * cosine + first_half * sine],
        axis=-1,
    )


def plain_layer(hidden_in, segment_ids, pre_gain, w_qkv, w_out, post_gain):
    tok_rows = hidden_in.shape[1]
    seq_count = lax.axis_size("seq")
    seq_index = lax.axis_index("seq")
    groups = Q_HEADS // KV_HEADS
    doc_most = min(WINDOW, seq_count * tok_rows // 8)
    hops = min(-(-(doc_most - 1) // tok_rows), seq_count - 1)
    positions = seq_index * tok_rows + jnp.arange(tok_rows, dtype=jnp.int32)
    own_ids = segment_ids[0]
    id_blocks = [from_behind(own_ids, "seq", d) for d in range(hops, 0, -1)] + [own_ids]
    widened = hidden_in[0].astype(jnp.float32)
    normed = rms_scale(widened, pre_gain).astype(jnp.bfloat16)
    projected = jnp.dot(
        normed,
        lax.all_gather(w_qkv, "seq", axis=0, tiled=True),
        preferred_element_type=jnp.float32,
    )
    queries = rotary(
        projected[:, : Q_HEADS * HEAD].reshape(tok_rows, KV_HEADS, groups, HEAD), positions, 0
    ).astype(jnp.bfloat16)
    key_rows = rotary(
        projected[:, Q_HEADS * HEAD : (Q_HEADS + KV_HEADS) * HEAD].reshape(
            tok_rows, KV_HEADS, HEAD
        ),
        positions,
        0,
    ).astype(jnp.bfloat16)
    value_rows = projected[:, (Q_HEADS + KV_HEADS) * HEAD :].astype(jnp.bfloat16)
    both = jnp.concatenate([key_rows.reshape(tok_rows, KV_HEADS * HEAD), value_rows], axis=1)
    blocks = [from_behind(both, "seq", d) for d in range(hops, 0, -1)] + [both]
    kv = jnp.concatenate(blocks, axis=0).reshape(-1, 2, KV_HEADS, HEAD)
    ids = jnp.concatenate(id_blocks, axis=0)
    key_pos = (seq_index - hops) * tok_rows + jnp.arange((hops + 1) * tok_rows, dtype=jnp.int32)
    allowed = (
        (key_pos[None, :] >= 0)
        & (key_pos[None, :] <= positions[:, None])
        & (positions[:, None] - key_pos[None, :] < WINDOW)
        & (ids[None, :] == own_ids[:, None])
    )
    scores = jnp.einsum(
        "qhgd,khd->hgqk", queries, kv[:, 0], preferred_element_type=jnp.float32
    ) * (1.0 / math.sqrt(HEAD))
    capped = CAP * jnp.tanh(scores / CAP)
    weights = jnp.where(allowed[None, None], jnp.exp(capped), 0.0)
    totals = jnp.sum(weights, axis=-1)
    mixed = jnp.einsum(
        "hgqk,khd->hgqd", weights.astype(jnp.bfloat16), kv[:, 1], preferred_element_type=jnp.float32
    )
    attended = (mixed / totals[..., None]).astype(jnp.bfloat16)
    attended = attended.transpose(2, 0, 1, 3).reshape(tok_rows, Q_HEADS * HEAD)
    branch = jnp.dot(
        attended,
        lax.all_gather(w_out, "seq", axis=0, tiled=True),
        preferred_element_type=jnp.float32,
    )
    return (widened + rms_scale(branch, post_gain)).astype(jnp.bfloat16)[None]


def split_rows(rows):
    first = (rows // 16 + 1) // 2 * 16
    return ((0, first), (first, rows - first))


class Ring:
    def __init__(self, place, classes, own_spot, full_spot, send_sems, recv_sems):
        self.place, self.classes = place, classes
        self.own_spot, self.full_spot = own_spot, full_spot
        self.send_sems, self.recv_sems = send_sems, recv_sems
        self.far = place["chips"] // 2
        self.near = place["chips"] - 1 - self.far
        self.relays = len(classes) * 2 * self.far
        self.extra = 2 * self.relays
        self.started = []

    def reach(self, piece, way):
        return self.far if self.classes[piece] == way else self.near

    def slot(self, piece, way, hop):
        return (piece * 2 + way) * self.far + hop - 1

    def origin(self, way, hop):
        return self.place["chip_at"](self.place["ring"] + (hop if way else -hop))

    def spot(self, piece, way, hop, core):
        return self.full_spot(piece, self.origin(way, hop) * 2 + core)

    def copy(self, source, target, slot, device):
        return pltpu.make_async_remote_copy(
            src_ref=source,
            dst_ref=target,
            send_sem=self.send_sems.at[slot],
            recv_sem=self.recv_sems.at[slot],
            device_id=device,
            device_id_type=pl.DeviceIdType.MESH,
        )

    def send(self, source, target, slot, device):
        moving = self.copy(source, target, slot, device)
        moving.start()
        self.started.append(moving)

    def arrived(self, spot, slot):
        self.copy(spot, spot, slot, self.place["sibling"]).wait_recv()

    def first(self, pieces):
        for piece in pieces:
            for way in (0, 1):
                self.send(
                    self.own_spot(piece),
                    self.full_spot(piece, self.place["seq"]),
                    self.slot(piece, way, 1),
                    self.place["onward"][way],
                )

    def step(self, hop, pieces, then=None):
        place = self.place
        for piece in pieces:
            for way in (0, 1):
                if hop > self.reach(piece, way):
                    continue
                spot = self.spot(piece, way, hop, place["core"])
                slot = self.slot(piece, way, hop)
                self.arrived(spot, slot)
                if hop < self.reach(piece, way):
                    self.send(spot, spot, slot + 1, place["onward"][way])
                if then is not None:
                    then(piece, way, hop, spot)
                self.send(spot, spot, self.relays + slot, place["sibling"])

    def relayed(self, pieces):
        other = 1 - self.place["core"]
        for piece in pieces:
            for way in (0, 1):
                for hop in range(1, self.reach(piece, way) + 1):
                    self.arrived(
                        self.spot(piece, way, hop, other), self.relays + self.slot(piece, way, hop)
                    )

    def drain(self):
        for moving in self.started:
            moving.wait_send()


def layer_kernel(
    chips, hid, ids, inverse_in, pre_in, w_qkv, w_out, post_in, result,
    ids0, inverse, pre, post, out, wq, wo, own, guest, nrm, qry, kv, kv1, kv2, ids1, far0, far1, near0, near1,
    cos, sin, acc, tot, att, attx, branch,
    q_send, q_recv, o_send, o_recv, s_send, s_recv, local_sem,
):
    seq, x = lax.axis_index("seq"), lax.axis_index("batch")
    chip, core = seq // 2, seq % 2
    half = chips // 2
    layer, side = chip // 2, chip % 2
    ring = (1 - side) * layer + side * (chips - 1 - layer)

    def chip_at(position):
        position = (position + chips) % chips
        far = position // half
        return (1 - far) * 2 * position + far * (2 * (chips - 1 - position) + 1)

    def at(device_chip, device_core, batch):
        return {"seq": device_chip * 2 + device_core, "batch": batch}

    up, down = at(chip_at(ring + 1), core, x), at(chip_at(ring - 1), core, x)
    sibling, across = at(chip, 1 - core, x), at(chip, core, 1 - x)
    after = at((chip + 1) % chips, core, x)
    before = at((chip + chips - 1) % chips, core, x)
    place = dict(
        chips=chips, seq=seq, core=core, ring=ring, chip_at=chip_at, sibling=sibling,
        onward=(up, down),
    )
    tokens, width = own.shape
    rows_q, rows_o = w_qkv.shape[0], w_out.shape[0]
    group = Q_HEADS // KV_HEADS
    third_width = width // 6

    def local(source, target, slot):
        moving = pltpu.make_async_copy(source, target, local_sem.at[slot])
        moving.start()
        return moving

    column_at = [
        (Q_HEADS + x) * HEAD, (Q_HEADS + KV_HEADS + x) * HEAD
    ] + [(group * x + head) * HEAD for head in range(group)]

    def columns_of(kind):
        return pl.ds(pl.multiple_of(column_at[kind], HEAD), HEAD)

    kinds = len(column_at)
    q_pieces = [(kind, start, count) for kind in range(kinds) for start, count in split_rows(rows_q)]

    def q_own(piece):
        kind, start, count = q_pieces[piece]
        return w_qkv.at[pl.ds(start, count), columns_of(kind)]

    def q_full(piece, device):
        kind, start, count = q_pieces[piece]
        return wq.at[kind, pl.ds(pl.multiple_of(device * rows_q + start, 16), count), :]

    def q_rows(kind, device):
        return wq.at[kind, pl.ds(pl.multiple_of(device * rows_q, 16), rows_q), :]

    def o_columns(third, unit):
        return pl.ds(pl.multiple_of((third * 2 + unit) * third_width, 128), third_width)

    def o_rows(device):
        return pl.ds(pl.multiple_of(device * rows_o, 16), rows_o)

    o_thirds = (2 * x, 1)

    def o_own(piece):
        return w_out.at[:, o_columns(o_thirds[piece % 2], piece // 2)]

    def o_full(piece, device):
        return wo.at[o_rows(device), o_columns(o_thirds[piece % 2], piece // 2)]

    gather_q = Ring(place, [kind % 2 for kind, _, _ in q_pieces], q_own, q_full, q_send, q_recv)
    gather_o = Ring(place, [0, 1, 0, 1], o_own, o_full, o_send, o_recv)

    ids_copy = local(ids, ids0, kinds + 2)
    own_copies = [local(hid, own, 0)]
    table_copies = [
        local(source, target, kinds + 3 + index)
        for index, (source, target) in enumerate(((inverse_in, inverse), (pre_in, pre), (post_in, post)))
    ]
    for kind in range(kinds):
        own_copies.append(local(w_qkv.at[:, columns_of(kind)], q_rows(kind, seq), kind + 1))
    own_copies.append(local(w_out, wo.at[o_rows(seq), :], kinds + 1))

    met = [sibling, across, up, down, after, before]
    barrier = pltpu.get_barrier_semaphore()
    for other in met:
        pl.semaphore_signal(barrier, 1, device_id=other, device_id_type=pl.DeviceIdType.MESH)
    ids_copy.wait()
    pl.semaphore_wait(barrier, len(met))

    def small(source, target, slot, device):
        return pltpu.make_async_remote_copy(
            src_ref=source, dst_ref=target, send_sem=s_send.at[slot], recv_sem=s_recv.at[slot],
            device_id=device, device_id_type=pl.DeviceIdType.MESH,
        )

    early = [piece for piece in range(len(q_pieces)) if q_pieces[piece][0] < 2]
    late = [piece for piece in range(len(q_pieces)) if q_pieces[piece][0] >= 2]
    crossers, others = (0, 2), (1, 3)
    o_pieces = crossers + others
    ids_across = small(ids0, ids1, 0, across)
    ids_across.start()
    ids_after = [small(ids0, far0, 1, after), small(ids1, far1, 2, after)]
    ids_after[0].start()
    gather_q.first(early)
    portion = tokens // 4
    guests = []
    for index in range(4):
        part = pl.ds(index * portion, portion)
        guests.append(small(hid.at[part, :], guest.at[part, :], 10 + index, across))
        guests[-1].start()
    for kind in range(kinds):
        gather_q.send(
            w_qkv.at[:, columns_of(kind)], q_rows(kind, seq), gather_q.extra + kind, sibling
        )
    gather_o.send(w_out, wo.at[o_rows(seq), :], gather_o.extra, sibling)

    strip = 16

    def normalize(source, base, start, count):
        @pl.loop(0, count // strip, unroll=2)
        def _(index):
            at_row = pl.multiple_of(start + index * strip, strip)
            values = source[pl.ds(at_row, strip), :].astype(jnp.float32)
            nrm[pl.ds(pl.multiple_of(base + at_row, strip), strip), :] = rms_scale(
                values, pre[...]
            ).astype(jnp.bfloat16)

    def pass_on(mine, far, near, slot):
        @pl.when(core == 0)
        def _():
            small(mine, near, slot, sibling).start()

        @pl.when(core == 1)
        def _():
            small(far, near, slot, sibling).start()

    def ids_near():
        ids_after[0].wait()
        ids_after[1].wait()
        pass_on(ids0, far0, near0, 3)
        pass_on(ids1, far1, near1, 4)

    def slot_rows(slot):
        return pl.ds(slot * tokens, tokens)

    def project(slot, kind):
        return jnp.dot(nrm[slot_rows(slot), :], wq[kind], preferred_element_type=jnp.float32)

    def turned(values):
        a, b = values[:, : HEAD // 2], values[:, HEAD // 2 :]
        c, s = cos[...], sin[...]
        return jnp.concatenate([a * c - b * s, b * c + a * s], axis=1).astype(jnp.bfloat16)

    def kv_moving(slot):
        return small(kv.at[slot_rows(slot), :], kv2.at[slot_rows(slot), :], 5 + slot, after)

    def make_kv(slot):
        kv[slot_rows(slot), :HEAD] = turned(project(slot, 0))
        kv[slot_rows(slot), HEAD:] = project(slot, 1).astype(jnp.bfloat16)

        @pl.when(chip < chips - 1)
        def _():
            kv_moving(slot).start()

    def take_kv(slot):
        @pl.when(chip > 0)
        def _():
            kv_moving(slot).wait_recv()

        rows = slot_rows(slot)
        pass_on(kv.at[rows, :], kv2.at[rows, :], kv1.at[rows, :], 7 + slot)

    def take_near(slot):
        rows = slot_rows(slot)
        small(kv.at[rows, :], kv1.at[rows, :], 7 + slot, sibling).wait()

    def make_queries(slot):
        for head in range(group):
            qry[slot_rows(slot), head * HEAD : (head + 1) * HEAD] = turned(project(slot, 2 + head))

    def take_guest(index):
        guests[index].wait()
        normalize(guest, tokens, index * portion, portion)

    def shared(kind):
        gather_q.arrived(q_rows(kind, seq + 1 - 2 * core), gather_q.extra + kind)

    def over(piece, way, hop, spot):
        if piece % 2 == 0:
            gather_o.send(spot, spot, crossing(piece, way, hop), across)

    def crossing(piece, way, hop):
        return gather_o.extra + 1 + ((piece // 2) * 2 + way) * gather_o.far + hop - 1

    crossings = 4 * gather_o.far

    def crossed_spot(piece, way, hop, on_core):
        device = gather_o.origin(way, hop) * 2 + on_core
        return wo.at[o_rows(device), o_columns(2 - 2 * x, piece // 2)]

    def crossed(hop, pieces):
        for piece in pieces:
            for way in (0, 1):
                if piece % 2 or hop > gather_o.reach(piece, way):
                    continue
                spot = crossed_spot(piece, way, hop, core)
                gather_o.arrived(spot, crossing(piece, way, hop))
                gather_o.send(spot, spot, crossings + crossing(piece, way, hop), sibling)

    def crossed_relayed(pieces):
        for piece in pieces:
            for way in (0, 1):
                if piece % 2:
                    continue
                for hop in range(1, gather_o.reach(piece, way) + 1):
                    gather_o.arrived(
                        crossed_spot(piece, way, hop, 1 - core),
                        crossings + crossing(piece, way, hop),
                    )

    row = lax.broadcasted_iota(jnp.int32, (tokens, tokens), 0)
    column = lax.broadcasted_iota(jnp.int32, (tokens, tokens), 1)

    def as_column(ids):
        spread = jnp.broadcast_to(ids[...], (tokens, tokens))
        return jnp.sum(jnp.where(row == column, spread, 0), axis=1, keepdims=True)

    def block(slot, head, source, allowed, first):
        rows = slot_rows(slot)
        columns = slice(head * HEAD, (head + 1) * HEAD)
        lanes = slice(head * 128, (head + 1) * 128)
        scores = lax.dot_general(
            qry[rows, columns], source[rows, :HEAD], (((1,), (1,)), ((), ())),
            preferred_element_type=jnp.float32,
        )
        bent = jnp.tanh(scores * (1.0 / (math.sqrt(HEAD) * CAP)))
        weights = jnp.where(allowed, jnp.exp2(bent * (CAP * math.log2(math.e))), 0.0)
        total = jnp.broadcast_to(jnp.sum(weights, axis=1, keepdims=True), (tokens, 128))
        mixed = jnp.dot(
            weights.astype(jnp.bfloat16), source[rows, HEAD:], preferred_element_type=jnp.float32
        )
        if first:
            acc[rows, columns] = mixed
            tot[rows, lanes] = total
        else:
            acc[rows, columns] += mixed
            tot[rows, lanes] += total

    def blocks(slot, source, allowed, first):
        for head in range(group):
            block(slot, head, source, allowed, first)

    def own_block(slot):
        ids = (ids0, ids1)[slot]
        blocks(slot, kv, (column <= row) & (as_column(ids) == ids[...]), True)

    def far_block(slot):
        ids = as_column((ids0, ids1)[slot])
        blocks(slot, kv2, (ids == (far0, far1)[slot][...]) & (row + seq >= row + 2), False)

    def near_block(slot):
        ids = as_column((ids0, ids1)[slot])
        blocks(slot, kv1, (ids == (near0, near1)[slot][...]) & (row + seq >= row + 1), False)
        rows = slot_rows(slot)
        for head in range(group):
            columns = slice(head * HEAD, (head + 1) * HEAD)
            att[rows, columns] = (acc[rows, columns] / tot[rows, head * 128 : head * 128 + 1]).astype(
                jnp.bfloat16
            )

    own_copies[0].wait()
    for moving in table_copies:
        moving.wait()
    normalize(own, 0, 0, tokens)
    gather_q.step(1, early)
    ids_across.wait()
    ids_after[1].start()
    positions = seq * tokens + lax.broadcasted_iota(jnp.int32, cos.shape, 0)
    angles = positions.astype(jnp.float32) * inverse[...]
    cos[...] = jnp.cos(angles)
    sin[...] = jnp.sin(angles)

    @pl.when(chip == 0)
    def _():
        kv2[...] = jnp.zeros_like(kv2)

    for hop in range(2, gather_q.near + 1):
        gather_q.step(hop, early)
    gather_q.first(late)
    for hop in range(gather_q.near + 1, gather_q.far + 1):
        gather_q.step(hop, early)
    gather_q.step(1, late)
    gather_o.first(crossers)
    for moving in own_copies[1:]:
        moving.wait()
    gather_q.relayed(early)
    shared(0)
    shared(1)
    make_kv(0)
    gather_q.step(2, late)
    take_guest(0)
    gather_o.step(1, crossers, over)
    take_guest(1)
    for hop in range(3, gather_q.near + 1):
        gather_q.step(hop, late)
    gather_o.step(2, crossers, over)
    take_guest(2)
    take_guest(3)
    make_kv(1)
    gather_o.first(others)
    ids_near()
    for hop in range(gather_q.near + 1, gather_q.far + 1):
        gather_q.step(hop, late)
    take_kv(0)
    for hop in range(3, gather_o.near + 1):
        gather_o.step(hop, crossers, over)
    gather_q.relayed(late)
    for kind in range(2, kinds):
        shared(kind)
    make_queries(0)
    make_queries(1)
    own_block(0)
    own_block(1)
    gather_o.step(1, others)
    small(ids0, near0, 3, sibling).wait()
    small(ids1, near1, 4, sibling).wait()
    far_block(0)
    take_near(0)
    near_block(0)
    for hop in range(gather_o.near + 1, gather_o.far + 1):
        gather_o.step(hop, crossers, over)
    gather_o.step(2, others)
    take_kv(1)
    far_block(1)
    take_near(1)
    near_block(1)
    att_moving = small(att.at[slot_rows(1), :], attx, 9, across)
    att_moving.start()
    for hop in range(3, gather_o.far + 1):
        gather_o.step(hop, others)
    for hop in range(1, gather_o.far + 1):
        crossed(hop, o_pieces)
    gather_o.relayed(o_pieces)
    crossed_relayed(o_pieces)
    gather_o.arrived(wo.at[o_rows(seq + 1 - 2 * core), :], gather_o.extra)
    mine_at = pl.ds(pl.multiple_of(x * group * HEAD, HEAD), group * HEAD)
    theirs_at = pl.ds(pl.multiple_of((1 - x) * group * HEAD, HEAD), group * HEAD)
    att_moving.wait()
    for start in range(0, width, 256):
        chunk = slice(start, start + 256)
        branch[:, chunk] = jnp.dot(
            att[slot_rows(0), :], wo[mine_at, chunk], preferred_element_type=jnp.float32
        ) + jnp.dot(attx[...], wo[theirs_at, chunk], preferred_element_type=jnp.float32)

    leaving = []
    for index in range(4):
        @pl.loop(index * portion // strip, (index + 1) * portion // strip, unroll=2)
        def _(step):
            rows = pl.ds(pl.multiple_of(step * strip, strip), strip)
            scaled = rms_scale(branch[rows, :], post[...])
            out[rows, :] = (own[rows, :].astype(jnp.float32) + scaled).astype(jnp.bfloat16)

        part = pl.ds(index * portion, portion)
        leaving.append(local(out.at[part, :], result.at[part, :], kinds + 6 + index))

    for slot in range(2):
        @pl.when(chip < chips - 1)
        def _():
            kv_moving(slot).wait_send()
    gather_q.drain()
    gather_o.drain()
    for moving in leaving:
        moving.wait()


def paired_layer(hidden_in, segment_ids, pre_gain, w_qkv, w_out, post_gain):
    tokens, width = hidden_in.shape[1:]
    chips = lax.axis_size("seq") // 2
    bf16, f32 = jnp.bfloat16, jnp.float32
    steps = np.arange(HEAD // 2, dtype=np.float32) * np.float32(2.0 / HEAD)
    inverse = np.float32(1.0) / np.float32(10000.0) ** steps
    vmem, dma = pltpu.VMEM, pltpu.SemaphoreType.DMA
    group = Q_HEADS // KV_HEADS
    heads = group * HEAD
    far = chips // 2
    q_sems = 2 * 2 * (2 + group) * 2 * far + 2 + group
    o_sems = 2 * 4 * 2 * far + 1 + 2 * 4 * far
    anywhere = pl.BlockSpec(memory_space=pl.ANY)
    result = pl.pallas_call(
        functools.partial(layer_kernel, chips),
        out_shape=jax.ShapeDtypeStruct((tokens, width), bf16),
        in_specs=[anywhere] * 7,
        out_specs=anywhere,
        scratch_shapes=[
            vmem((1, tokens), jnp.int32),
            vmem((1, HEAD // 2), f32),
            vmem((width,), f32),
            vmem((width,), f32),
            vmem((tokens, width), bf16),
            vmem((2 + group, width, HEAD), bf16),
            vmem((w_out.shape[0] * chips * 2, width), bf16),
            vmem((tokens, width), bf16),
            vmem((tokens, width), bf16),
            vmem((2 * tokens, width), bf16),
            vmem((2 * tokens, heads), bf16),
            vmem((2 * tokens, 2 * HEAD), bf16),
            vmem((2 * tokens, 2 * HEAD), bf16),
            vmem((2 * tokens, 2 * HEAD), bf16),
            vmem((1, tokens), jnp.int32),
            vmem((1, tokens), jnp.int32),
            vmem((1, tokens), jnp.int32),
            vmem((1, tokens), jnp.int32),
            vmem((1, tokens), jnp.int32),
            vmem((tokens, HEAD // 2), f32),
            vmem((tokens, HEAD // 2), f32),
            vmem((2 * tokens, heads), f32),
            vmem((2 * tokens, group * 128), f32),
            vmem((2 * tokens, heads), bf16),
            vmem((tokens, heads), bf16),
            vmem((tokens, width), f32),
            dma((q_sems,)),
            dma((q_sems,)),
            dma((o_sems,)),
            dma((o_sems,)),
            dma((14,)),
            dma((14,)),
            dma((12 + group,)),
        ],
        compiler_params=pltpu.CompilerParams(
            collective_id=0, has_side_effects=True, vmem_limit_bytes=58 * 1024 * 1024
        ),
    )(
        hidden_in[0],
        segment_ids,
        jnp.asarray(inverse)[None, :],
        pre_gain,
        w_qkv,
        w_out,
        post_gain,
    )
    return result[None]


def per_device(hidden_in, segment_ids, pre_gain, w_qkv, w_out, post_gain):
    tokens, width = hidden_in.shape[1:]
    seq_count = lax.axis_size("seq")
    doc_most = min(WINDOW, seq_count * tokens // 8)
    whole_tiles = w_qkv.shape[0] % 16 == 0 and w_out.shape[0] % 16 == 0 and width % 768 == 0
    two_hops = doc_most - 1 <= 2 * tokens and 3 * tokens <= WINDOW
    small_ring = seq_count % 4 == 0 and seq_count > 12
    if whole_tiles and two_hops and small_ring and lax.axis_size("batch") == 2 and KV_HEADS == 2:
        layer = paired_layer
    else:
        layer = plain_layer
    return layer(hidden_in, segment_ids, pre_gain, w_qkv, w_out, post_gain)


def solution(mesh):
    placed = (P("batch", "seq", None), P("batch", "seq"), P(), P("seq", None), P("seq", None), P())
    return jax.shard_map(
        per_device, mesh=mesh, in_specs=placed, out_specs=P("batch", "seq", None), check_vma=False
    )
```

time: 88.5 us -> 75.4 us (0.85)
  Pallas kernels: 83.2 us -> 72.9 us
  local copies, waits for them, and re-layouts: 3.8 us -> 2.36 us
  other arithmetic: 1.26 us -> 0 us
    pallas_call x1, Pallas kernels: 83.2 us -> 72.9 us  [paired_layer(): pl.pallas_call(functools.partial(layer_kernel, chips), out_shape=jax.Shap...]
    broadcast_in_dim x1 -> x0, local copies, waits for them, and re-layouts: 1.44 us -> none  [ring_layer(): jnp.broadcast_to(ids[:, None], (tokens, 128))]
    sin x1 -> x0, other arithmetic: 1.25 us -> none  [ring_layer(): jnp.sin(angles)]
where the time goes in v1:
time: 75.4 us; the launch traced here: 75.2 us
  Pallas kernels  72.9 us (97%)
  local copies, waits for them, and re-layouts  2.36 us (3%)
    pallas_call x1, Pallas kernels, paired_layer(): pl.pallas_call(functools.partial(layer_kernel, chips), out_shape=jax.Shap...  72.9 us
    unnamed x1, local copies, waits for them, and re-layouts  2.36 us

profile of v1, /device:TPU:0, one launch (start us, length us, event | category | flops | bytes accessed | tf_op | source)
XLA Modules:
  0.0 75.2 jit_solution(12229043488682506438)
XLA Ops:
  0.0 72.9 %shard_map.73 = bf16[256,2304]{1,0:T(8,128)(2,1)} custom-call(bf16[256,2304]{1,0:T(8,128)(2,1)} %bitcast.3, s32[1,256]{1,0:T(1,128)} %ids.1, f32[1,128]{1,0:T(1,128)} %constant.5.inverse_in, f32[2304]{0:T(1024)} %pre_in.1, bf16[144,2048]{1,0:T(8,128)(2,1)} %w_qkv.1, bf16[64,2304]{1,0:T(8,128)(2,1)} %w_out.1, f32[2304]{0:T(1024)} %post_in.1), custom_call_target="tpu_custom_call" | custom-call | tf_op jit(solution)/shard_map/pallas_call | solution.py:586
  72.9 2.4 %copy.9 = bf16[1,256,2304]{2,1,0:T(8,128)(2,1)} copy(bf16[1,256,2304]{2,1,0:T(8,128)(2,1)} %bitcast.2) | data formatting | bytes 2359296

commit v2 on v1

--- a/solution.py
+++ b/solution.py
@@ -112,45 +112,45 @@
 
 
 class Ring:
-    def __init__(self, place, classes, own_spot, full_spot, send_sems, recv_sems):
+    def __init__(self, place, classes, own_spot, full_spot, send_sem, recv_sems):
         self.place, self.classes = place, classes
         self.own_spot, self.full_spot = own_spot, full_spot
-        self.send_sems, self.recv_sems = send_sems, recv_sems
+        self.send_sem, self.recv_sems = send_sem, recv_sems
         self.far = place["chips"] // 2
         self.near = place["chips"] - 1 - self.far
-        self.relays = len(classes) * 2 * self.far
-        self.extra = 2 * self.relays
-        self.started = []
+        self.extra = len(classes) * (self.far + self.near)
 
     def reach(self, piece, way):
         return self.far if self.classes[piece] == way else self.near
 
     def slot(self, piece, way, hop):
-        return (piece * 2 + way) * self.far + hop - 1
+        onset = 0 if self.classes[piece] == way else self.far
+        return piece * (self.far + self.near) + onset + hop - 1
 
     def origin(self, way, hop):
         return self.place["chip_at"](self.place["ring"] + (hop if way else -hop))
 
-    def spot(self, piece, way, hop, core):
-        return self.full_spot(piece, self.origin(way, hop) * 2 + core)
+    def spot(self, piece, way, hop):
+        return self.full_spot(piece, self.origin(way, hop) * 2 + self.place["core"])
 
     def copy(self, source, target, slot, device):
         return pltpu.make_async_remote_copy(
             src_ref=source,
             dst_ref=target,
-            send_sem=self.send_sems.at[slot],
+            send_sem=self.send_sem.at[0],
             recv_sem=self.recv_sems.at[slot],
             device_id=device,
             device_id_type=pl.DeviceIdType.MESH,
         )
 
     def send(self, source, target, slot, device):
-        moving = self.copy(source, target, slot, device)
-        moving.start()
-        self.started.append(moving)
+        self.copy(source, target, slot, device).start()
 
     def arrived(self, spot, slot):
         self.copy(spot, spot, slot, self.place["sibling"]).wait_recv()
+
+    def sent(self, as_much):
+        self.copy(as_much, as_much, 0, self.place["sibling"]).wait_send()
 
     def first(self, pieces):
         for piece in pieces:
@@ -162,39 +162,26 @@
                     self.place["onward"][way],
                 )
 
-    def step(self, hop, pieces, then=None):
+    def step(self, hop, pieces, relay_slot, then=None):
         place = self.place
         for piece in pieces:
             for way in (0, 1):
                 if hop > self.reach(piece, way):
                     continue
-                spot = self.spot(piece, way, hop, place["core"])
+                spot = self.spot(piece, way, hop)
                 slot = self.slot(piece, way, hop)
                 self.arrived(spot, slot)
                 if hop < self.reach(piece, way):
                     self.send(spot, spot, slot + 1, place["onward"][way])
                 if then is not None:
                     then(piece, way, hop, spot)
-                self.send(spot, spot, self.relays + slot, place["sibling"])
-
-    def relayed(self, pieces):
-        other = 1 - self.place["core"]
-        for piece in pieces:
-            for way in (0, 1):
-                for hop in range(1, self.reach(piece, way) + 1):
-                    self.arrived(
-                        self.spot(piece, way, hop, other), self.relays + self.slot(piece, way, hop)
-                    )
-
-    def drain(self):
-        for moving in self.started:
-            moving.wait_send()
+                self.send(spot, spot, relay_slot, place["sibling"])
 
 
 def layer_kernel(
-    chips, hid, ids, inverse_in, pre_in, w_qkv, w_out, post_in, result,
-    ids0, inverse, pre, post, out, wq, wo, own, guest, nrm, qry, kv, kv1, kv2, ids1, far0, far1, near0, near1,
-    cos, sin, acc, tot, att, attx, branch,
+    chips, hid, ids, inverse_in, pre_in, w_qkv, w_out, own, branch,
+    ids0, inverse, pre, wq, wo, guest, nrm, qry, kv, kv1, kv2, ids1, far0, far1, near0, near1,
+    cos, sin, acc, tot, att, attx,
     q_send, q_recv, o_send, o_recv, s_send, s_recv, local_sem,
 ):
     seq, x = lax.axis_index("seq"), lax.axis_index("batch")
@@ -271,7 +258,7 @@
     own_copies = [local(hid, own, 0)]
     table_copies = [
         local(source, target, kinds + 3 + index)
-        for index, (source, target) in enumerate(((inverse_in, inverse), (pre_in, pre), (post_in, post)))
+        for index, (source, target) in enumerate(((inverse_in, inverse), (pre_in, pre)))
     ]
     for kind in range(kinds):
         own_copies.append(local(w_qkv.at[:, columns_of(kind)], q_rows(kind, seq), kind + 1))
@@ -293,6 +280,7 @@
     early = [piece for piece in range(len(q_pieces)) if q_pieces[piece][0] < 2]
     late = [piece for piece in range(len(q_pieces)) if q_pieces[piece][0] >= 2]
     crossers, others = (0, 2), (1, 3)
+    early_relay, late_relay, o_relay = gather_q.extra, gather_q.extra + 1, gather_o.extra
     o_pieces = crossers + others
     ids_across = small(ids0, ids1, 0, across)
     ids_across.start()
@@ -307,9 +295,9 @@
         guests[-1].start()
     for kind in range(kinds):
         gather_q.send(
-            w_qkv.at[:, columns_of(kind)], q_rows(kind, seq), gather_q.extra + kind, sibling
+            w_qkv.at[:, columns_of(kind)], q_rows(kind, seq), early_relay + (kind >= 2), sibling
         )
-    gather_o.send(w_out, wo.at[o_rows(seq), :], gather_o.extra, sibling)
+    gather_o.send(w_out, wo.at[o_rows(seq), :], o_relay, sibling)
 
     strip = 16
 
@@ -355,6 +343,7 @@
         kv[slot_rows(slot), :HEAD] = turned(project(slot, 0))
         kv[slot_rows(slot), HEAD:] = project(slot, 1).astype(jnp.bfloat16)
 
+    def send_kv(slot):
         @pl.when(chip < chips - 1)
         def _():
             kv_moving(slot).start()
@@ -379,41 +368,23 @@
         guests[index].wait()
         normalize(guest, tokens, index * portion, portion)
 
-    def shared(kind):
-        gather_q.arrived(q_rows(kind, seq + 1 - 2 * core), gather_q.extra + kind)
-
     def over(piece, way, hop, spot):
-        if piece % 2 == 0:
+        if piece in crossers:
             gather_o.send(spot, spot, crossing(piece, way, hop), across)
 
     def crossing(piece, way, hop):
-        return gather_o.extra + 1 + ((piece // 2) * 2 + way) * gather_o.far + hop - 1
-
-    crossings = 4 * gather_o.far
-
-    def crossed_spot(piece, way, hop, on_core):
-        device = gather_o.origin(way, hop) * 2 + on_core
-        return wo.at[o_rows(device), o_columns(2 - 2 * x, piece // 2)]
+        first = crossers.index(piece) - piece
+        return o_relay + 1 + first * (chips - 1) + gather_o.slot(piece, way, hop)
 
     def crossed(hop, pieces):
         for piece in pieces:
             for way in (0, 1):
-                if piece % 2 or hop > gather_o.reach(piece, way):
+                if hop > gather_o.reach(piece, way):
                     continue
-                spot = crossed_spot(piece, way, hop, core)
+                device = gather_o.origin(way, hop) * 2 + core
+                spot = wo.at[o_rows(device), o_columns(2 - 2 * x, piece // 2)]
                 gather_o.arrived(spot, crossing(piece, way, hop))
-                gather_o.send(spot, spot, crossings + crossing(piece, way, hop), sibling)
-
-    def crossed_relayed(pieces):
-        for piece in pieces:
-            for way in (0, 1):
-                if piece % 2:
-                    continue
-                for hop in range(1, gather_o.reach(piece, way) + 1):
-                    gather_o.arrived(
-                        crossed_spot(piece, way, hop, 1 - core),
-                        crossings + crossing(piece, way, hop),
-                    )
+                gather_o.send(spot, spot, o_relay, sibling)
 
     row = lax.broadcasted_iota(jnp.int32, (tokens, tokens), 0)
     column = lax.broadcasted_iota(jnp.int32, (tokens, tokens), 1)
@@ -469,7 +440,7 @@
     for moving in table_copies:
         moving.wait()
     normalize(own, 0, 0, tokens)
-    gather_q.step(1, early)
+    gather_q.step(1, early, early_relay)
     ids_across.wait()
     ids_after[1].start()
     positions = seq * tokens + lax.broadcasted_iota(jnp.int32, cos.shape, 0)
@@ -481,74 +452,89 @@
     def _():
         kv2[...] = jnp.zeros_like(kv2)
 
-    for hop in range(2, gather_q.near + 1):
-        gather_q.step(hop, early)
+    gather_q.step(2, early, early_relay)
     gather_q.first(late)
-    for hop in range(gather_q.near + 1, gather_q.far + 1):
-        gather_q.step(hop, early)
-    gather_q.step(1, late)
-    gather_o.first(crossers)
+    for hop in range(3, gather_q.near + 1):
+        gather_q.step(hop, early, early_relay)
     for moving in own_copies[1:]:
         moving.wait()
-    gather_q.relayed(early)
-    shared(0)
-    shared(1)
+    for hop in range(gather_q.near + 1, gather_q.far + 1):
+        gather_q.step(hop, early, early_relay)
+    gather_o.first(crossers)
+    gather_q.step(1, late, late_relay)
+    gather_q.arrived(wq.at[:2, : chips * rows_q, :], early_relay)
+    gather_o.first(others)
     make_kv(0)
-    gather_q.step(2, late)
+    gather_q.step(2, late, late_relay)
     take_guest(0)
-    gather_o.step(1, crossers, over)
+    gather_o.step(1, crossers, o_relay, over)
     take_guest(1)
     for hop in range(3, gather_q.near + 1):
-        gather_q.step(hop, late)
-    gather_o.step(2, crossers, over)
+        gather_q.step(hop, late, late_relay)
+    gather_o.step(1, others, o_relay)
     take_guest(2)
     take_guest(3)
     make_kv(1)
-    gather_o.first(others)
+    send_kv(1)
+    gather_o.step(2, crossers, o_relay, over)
+    send_kv(0)
+    gather_o.step(2, others, o_relay)
     ids_near()
     for hop in range(gather_q.near + 1, gather_q.far + 1):
-        gather_q.step(hop, late)
-    take_kv(0)
-    for hop in range(3, gather_o.near + 1):
-        gather_o.step(hop, crossers, over)
-    gather_q.relayed(late)
-    for kind in range(2, kinds):
-        shared(kind)
+        gather_q.step(hop, late, late_relay)
+    gather_q.arrived(wq.at[2:, : chips * rows_q, :], late_relay)
+    make_queries(1)
+    own_block(1)
     make_queries(0)
-    make_queries(1)
     own_block(0)
-    own_block(1)
-    gather_o.step(1, others)
     small(ids0, near0, 3, sibling).wait()
     small(ids1, near1, 4, sibling).wait()
-    far_block(0)
-    take_near(0)
-    near_block(0)
-    for hop in range(gather_o.near + 1, gather_o.far + 1):
-        gather_o.step(hop, crossers, over)
-    gather_o.step(2, others)
     take_kv(1)
     far_block(1)
+    for hop in range(3, gather_o.near + 1):
+        gather_o.step(hop, crossers, o_relay, over)
     take_near(1)
     near_block(1)
     att_moving = small(att.at[slot_rows(1), :], attx, 9, across)
     att_moving.start()
-    for hop in range(3, gather_o.far + 1):
-        gather_o.step(hop, others)
-    for hop in range(1, gather_o.far + 1):
-        crossed(hop, o_pieces)
-    gather_o.relayed(o_pieces)
-    crossed_relayed(o_pieces)
-    gather_o.arrived(wo.at[o_rows(seq + 1 - 2 * core), :], gather_o.extra)
+    for hop in range(3, gather_o.near + 1):
+        gather_o.step(hop, others, o_relay)
+    take_kv(0)
+    far_block(0)
+    for hop in range(gather_o.near + 1, gather_o.far + 1):
+        gather_o.step(hop, crossers, o_relay, over)
+    take_near(0)
+    near_block(0)
+    for hop in range(1, gather_o.far):
+        crossed(hop, crossers)
+    for hop in range(gather_o.near + 1, gather_o.far + 1):
+        gather_o.step(hop, others, o_relay)
+    crossed(gather_o.far, crossers)
+    gather_o.arrived(wo.at[: chips * rows_o, :], o_relay)
     mine_at = pl.ds(pl.multiple_of(x * group * HEAD, HEAD), group * HEAD)
     theirs_at = pl.ds(pl.multiple_of((1 - x) * group * HEAD, HEAD), group * HEAD)
-    att_moving.wait()
-    for start in range(0, width, 256):
-        chunk = slice(start, start + 256)
+    chunks = [slice(start, start + 256) for start in range(0, width, 256)]
+    for chunk in chunks:
         branch[:, chunk] = jnp.dot(
             att[slot_rows(0), :], wo[mine_at, chunk], preferred_element_type=jnp.float32
-        ) + jnp.dot(attx[...], wo[theirs_at, chunk], preferred_element_type=jnp.float32)
-
+        )
+    att_moving.wait()
+    for chunk in chunks:
+        branch[:, chunk] += jnp.dot(
+            attx[...], wo[theirs_at, chunk], preferred_element_type=jnp.float32
+        )
+
+    for slot in range(2):
+        @pl.when(chip < chips - 1)
+        def _():
+            kv_moving(slot).wait_send()
+    gather_q.sent(wq.at[:, : (2 * chips - 1) * rows_q, :])
+    gather_o.sent(wo.at[: (2 * chips - 1) * rows_o, :])
+
+
+def finish_kernel(own, branch, post, result, out, sems):
+    tokens = own.shape[0]
+    strip, portion = 16, tokens // 4
     leaving = []
     for index in range(4):
         @pl.loop(index * portion // strip, (index + 1) * portion // strip, unroll=2)
@@ -558,14 +544,8 @@
             out[rows, :] = (own[rows, :].astype(jnp.float32) + scaled).astype(jnp.bfloat16)
 
         part = pl.ds(index * portion, portion)
-        leaving.append(local(out.at[part, :], result.at[part, :], kinds + 6 + index))
-
-    for slot in range(2):
-        @pl.when(chip < chips - 1)
-        def _():
-            kv_moving(slot).wait_send()
-    gather_q.drain()
-    gather_o.drain()
+        leaving.append(pltpu.make_async_copy(out.at[part, :], result.at[part, :], sems.at[index]))
+        leaving[-1].start()
     for moving in leaving:
         moving.wait()
 
@@ -579,24 +559,21 @@
     vmem, dma = pltpu.VMEM, pltpu.SemaphoreType.DMA
     group = Q_HEADS // KV_HEADS
     heads = group * HEAD
-    far = chips // 2
-    q_sems = 2 * 2 * (2 + group) * 2 * far + 2 + group
-    o_sems = 2 * 4 * 2 * far + 1 + 2 * 4 * far
+    q_sems = 2 * (2 + group) * (chips - 1) + 2
+    o_sems = 6 * (chips - 1) + 1
     anywhere = pl.BlockSpec(memory_space=pl.ANY)
-    result = pl.pallas_call(
+    in_vmem = pl.BlockSpec(memory_space=vmem)
+    own, branch = pl.pallas_call(
         functools.partial(layer_kernel, chips),
-        out_shape=jax.ShapeDtypeStruct((tokens, width), bf16),
-        in_specs=[anywhere] * 7,
-        out_specs=anywhere,
+        out_shape=(vmem((tokens, width), bf16), vmem((tokens, width), f32)),
+        in_specs=[anywhere] * 6,
+        out_specs=(in_vmem, in_vmem),
         scratch_shapes=[
             vmem((1, tokens), jnp.int32),
             vmem((1, HEAD // 2), f32),
             vmem((width,), f32),
-            vmem((width,), f32),
-            vmem((tokens, width), bf16),
             vmem((2 + group, width, HEAD), bf16),
             vmem((w_out.shape[0] * chips * 2, width), bf16),
-            vmem((tokens, width), bf16),
             vmem((tokens, width), bf16),
             vmem((2 * tokens, width), bf16),
             vmem((2 * tokens, heads), bf16),
@@ -614,14 +591,13 @@
             vmem((2 * tokens, group * 128), f32),
             vmem((2 * tokens, heads), bf16),
             vmem((tokens, heads), bf16),
-            vmem((tokens, width), f32),
+            dma((1,)),
             dma((q_sems,)),
-            dma((q_sems,)),
-            dma((o_sems,)),
+            dma((1,)),
             dma((o_sems,)),
             dma((14,)),
             dma((14,)),
-            dma((12 + group,)),
+            dma((7 + group,)),
         ],
         compiler_params=pltpu.CompilerParams(
             collective_id=0, has_side_effects=True, vmem_limit_bytes=58 * 1024 * 1024
@@ -633,6 +609,17 @@
         pre_gain,
         w_qkv,
         w_out,
+    )
+    result = pl.pallas_call(
+        finish_kernel,
+        out_shape=jax.ShapeDtypeStruct((tokens, width), bf16),
+        in_specs=[in_vmem] * 3,
+        out_specs=anywhere,
+        scratch_shapes=[vmem((tokens, width), bf16), dma((4,))],
+        compiler_params=pltpu.CompilerParams(vmem_limit_bytes=12 * 1024 * 1024),
+    )(
+        pltpu.with_memory_space_constraint(own, vmem),
+        pltpu.with_memory_space_constraint(branch, vmem),
         post_gain,
     )
     return result[None]

time: 75.4 us -> 67.9 us (0.901)
  the two profiles are of different devices: /device:TPU:0 before, /device:TPU:25 now
where the time goes in v2:
time: 67.9 us; the launch traced here: 67.8 us
  Pallas kernels  67.7 us (100%)
    pallas_call x1, Pallas kernels, paired_layer(): pl.pallas_call(functools.partial(layer_kernel, chips), out_shape=(vmem((t...  65.8 us
    pallas_call x1, Pallas kernels, paired_layer(): pl.pallas_call(finish_kernel, out_shape=jax.ShapeDtypeStruct((tokens, wid...  1.96 us

profile of v2, /device:TPU:25, one launch (start us, length us, event | category | flops | bytes accessed | tf_op | source)
XLA Modules:
  0.0 67.8 jit_solution(11813879169608746627)
XLA Ops:
  0.0 0.0 copy-start
  0.0 65.8 %shard_map.73 = (bf16[256,2304]{1,0:T(8,128)(2,1)S(1)}, f32[256,2304]{1,0:T(8,128)S(1)}) custom-call(bf16[256,2304]{1,0:T(8,128)(2,1)} %bitcast.2, s32[1,256]{1,0:T(1,128)} %ids.1, f32[1,128]{1,0:T(1,128)} %constant.5.inverse_in, f32[2304]{0:T(1024)} %pre_in.1, bf16[144,2048]{1,0:T(8,128)(2,1)} %w_qkv.1, bf16[64,2304]{1,0:T(8,128)(2,1)} %w_out.1), custom_call_target="tpu_custom_call" | custom-call | tf_op jit(solution)/shard_map/pallas_call | solution.py:566
  65.8 0.0 copy-done
  65.8 2.0 %shard_map.74 = bf16[256,2304]{1,0:T(8,128)(2,1)} custom-call(bf16[256,2304]{1,0:T(8,128)(2,1)S(1)} %get-tuple-element.7.own, f32[256,2304]{1,0:T(8,128)S(1)} %get-tuple-element.8.branch, f32[2304]{0:T(1024)S(1)} %copy-done), custom_call_target="tpu_custom_call" | custom-call | tf_op jit(solution)/shard_map/pallas_call | solution.py:613
Async XLA Ops:
  0.0 65.8 %copy-start = (f32[2304]{0:T(1024)S(1)}, f32[2304]{0:T(1024)}, u32[]{:S(2)}) copy-start(f32[2304]{0:T(1024)} %post.1) | copy-start | bytes 27652

commit v3 on v2

--- a/solution.py
+++ b/solution.py
@@ -469,47 +469,42 @@
     take_guest(0)
     gather_o.step(1, crossers, o_relay, over)
     take_guest(1)
-    for hop in range(3, gather_q.near + 1):
-        gather_q.step(hop, late, late_relay)
-    gather_o.step(1, others, o_relay)
+    gather_q.step(3, late, late_relay)
     take_guest(2)
     take_guest(3)
     make_kv(1)
     send_kv(1)
+    gather_o.step(1, others, o_relay)
     gather_o.step(2, crossers, o_relay, over)
     send_kv(0)
-    gather_o.step(2, others, o_relay)
     ids_near()
-    for hop in range(gather_q.near + 1, gather_q.far + 1):
-        gather_q.step(hop, late, late_relay)
+    gather_q.step(4, late, late_relay)
     gather_q.arrived(wq.at[2:, : chips * rows_q, :], late_relay)
     make_queries(1)
     own_block(1)
     make_queries(0)
     own_block(0)
+    gather_o.step(2, others, o_relay)
     small(ids0, near0, 3, sibling).wait()
     small(ids1, near1, 4, sibling).wait()
     take_kv(1)
     far_block(1)
-    for hop in range(3, gather_o.near + 1):
-        gather_o.step(hop, crossers, o_relay, over)
+    gather_o.step(3, crossers, o_relay, over)
     take_near(1)
     near_block(1)
     att_moving = small(att.at[slot_rows(1), :], attx, 9, across)
     att_moving.start()
-    for hop in range(3, gather_o.near + 1):
-        gather_o.step(hop, others, o_relay)
+    gather_o.step(3, others, o_relay)
     take_kv(0)
     far_block(0)
-    for hop in range(gather_o.near + 1, gather_o.far + 1):
-        gather_o.step(hop, crossers, o_relay, over)
+    gather_o.step(4, crossers, o_relay, over)
     take_near(0)
     near_block(0)
-    for hop in range(1, gather_o.far):
-        crossed(hop, crossers)
-    for hop in range(gather_o.near + 1, gather_o.far + 1):
-        gather_o.step(hop, others, o_relay)
-    crossed(gather_o.far, crossers)
+    crossed(1, crossers)
+    crossed(2, crossers)
+    crossed(3, crossers)
+    gather_o.step(4, others, o_relay)
+    crossed(4, crossers)
     gather_o.arrived(wo.at[: chips * rows_o, :], o_relay)
     mine_at = pl.ds(pl.multiple_of(x * group * HEAD, HEAD), group * HEAD)
     theirs_at = pl.ds(pl.multiple_of((1 - x) * group * HEAD, HEAD), group * HEAD)

time: 67.9 us -> 64.6 us (0.951)
  the two profiles are of different devices: /device:TPU:25 before, /device:TPU:5 now
where the time goes in v3:
time: 64.6 us; the launch traced here: 64.5 us
  Pallas kernels  64.5 us (100%)
    pallas_call x1, Pallas kernels, paired_layer(): pl.pallas_call(functools.partial(layer_kernel, chips), out_shape=(vmem((t...  62.5 us
    pallas_call x1, Pallas kernels, paired_layer(): pl.pallas_call(finish_kernel, out_shape=jax.ShapeDtypeStruct((tokens, wid...  1.96 us

profile of v3, /device:TPU:5, one launch (start us, length us, event | category | flops | bytes accessed | tf_op | source)
XLA Modules:
  0.0 64.5 jit_solution(2005117982788064526)
XLA Ops:
  0.0 0.0 copy-start
  0.0 62.5 %shard_map.73 = (bf16[256,2304]{1,0:T(8,128)(2,1)S(1)}, f32[256,2304]{1,0:T(8,128)S(1)}) custom-call(bf16[256,2304]{1,0:T(8,128)(2,1)} %bitcast.2, s32[1,256]{1,0:T(1,128)} %ids.1, f32[1,128]{1,0:T(1,128)} %constant.5.inverse_in, f32[2304]{0:T(1024)} %pre_in.1, bf16[144,2048]{1,0:T(8,128)(2,1)} %w_qkv.1, bf16[64,2304]{1,0:T(8,128)(2,1)} %w_out.1), custom_call_target="tpu_custom_call" | custom-call | tf_op jit(solution)/shard_map/pallas_call | solution.py:561
  62.5 0.0 copy-done
  62.5 2.0 %shard_map.74 = bf16[256,2304]{1,0:T(8,128)(2,1)} custom-call(bf16[256,2304]{1,0:T(8,128)(2,1)S(1)} %get-tuple-element.7.own, f32[256,2304]{1,0:T(8,128)S(1)} %get-tuple-element.8.branch, f32[2304]{0:T(1024)S(1)} %copy-done), custom_call_target="tpu_custom_call" | custom-call | tf_op jit(solution)/shard_map/pallas_call | solution.py:608
Async XLA Ops:
  0.0 62.5 %copy-start = (f32[2304]{0:T(1024)S(1)}, f32[2304]{0:T(1024)}, u32[]{:S(2)}) copy-start(f32[2304]{0:T(1024)} %post.1) | copy-start | bytes 27652
